TPU v7x, 32 devices: a whole 2x2x4 slice. The times are simulated.
32 devices in a mesh: wide: 2 (over x), narrow: 4 (over y, core), depth: 4 (over z).
Axes of the slice: x: 2, y: 2, z: 4, core: 2. Of those that a mesh axis runs over, the one named last changes fastest.
Arguments:
- patch_store: bfloat16 [8, 1024, 4096], P('wide', 'depth'), may hold values from -6 to 6
- w_key: bfloat16 [4096, 1024], P(None, 'narrow'), may hold values from -0.09375 to 0.09375
- w_value: bfloat16 [4096, 1024], P(None, 'narrow'), may hold values from -0.09375 to 0.09375
- key_gain: float32 [128], replicated, may hold values from 0.1 to 1.9
- query_gain: float32 [128], replicated, may hold values from 0.1 to 1.9
- queries: bfloat16 [32, 4096], P('wide', 'narrow'), may hold values from -6 to 6
- owner_table: int32 [8], replicated, may hold values from 0 to 7, each once
- reader_table: int32 [2, 2], replicated, may hold values from 0 to 7
- request_image: int32 [32], P('wide'), may hold values from 0 to 1
- image_tiles: int32 [8], replicated, may hold values from 1 to 4
Outputs:
- context: bfloat16 [32, 4096], P(('wide', 'depth'), 'narrow')
Inputs may be any that keep to these rules, and one draw needn't show every extreme that they name: owner_table is a permutation of the slots. `reader_table`: entries are image ids; a group's list may repeat an image.
All inputs are finite; a program needn't handle non-finite values.
Results may differ from a plain program's by a relative error of at most 0.012.
Values may be sent and summed in bfloat16 or wider, within the bound.
A program may use at most 64 MiB of HBM per device.

v0:
```python
import functools
import math

import jax
import jax.numpy as jnp
from jax import lax
from jax.experimental import pallas as pl
from jax.experimental.pallas import tpu as pltpu
from jax.sharding import PartitionSpec as P

HD = 128
TILE_P = 256
EPSILON = 1e-05
CHUNKS = 4
MEET = 0
MESH = pl.DeviceIdType.MESH


def kernel(
    n_wide,
    n_depth,
    store,
    w_key,
    w_value,
    key_gain,
    query_gain,
    queries,
    owner_hbm,
    reader_hbm,
    request_hbm,
    tiles_hbm,
    out,
    owner_table,
    reader_table,
    request_image,
    image_tiles,
    xbuf,
    wbuf,
    qraw,
    gains,
    qf,
    qs,
    qx,
    row_slot,
    row_limit,
    raw,
    keys,
    values,
    msg,
    got,
    res,
    w_sem,
    x_sem,
    q_sem,
    q_send,
    q_recv,
    m_send,
    m_recv,
):
    images, rows, width = xbuf.shape
    kv_local = wbuf.shape[0]
    batch = qraw.shape[0]
    group = qraw.shape[1] // (kv_local * HD)
    share = batch // n_depth
    block = share * group
    group_rows = n_depth * block
    peers = n_wide * n_depth
    total_rows = peers * block
    chunk = width // CHUNKS
    wide, depth = lax.axis_index("wide"), lax.axis_index("depth")
    me = wide * n_depth + depth
    part_lanes = HD // kv_local

    barrier = pltpu.get_barrier_semaphore()

    def peer(offset):
        there = {
            "wide": lax.rem(wide + offset // n_depth, n_wide),
            "depth": lax.rem(depth + offset % n_depth, n_depth),
        }
        return there["wide"] * n_depth + there["depth"], there

    def greet(offset, carry):
        pl.semaphore_signal(barrier, inc=1, device_id=peer(offset)[1], device_id_type=MESH)
        return carry

    lax.fori_loop(1, peers, greet, 0, unroll=peers <= 8)

    def weight_copies(k, c):
        piece = pl.ds(c * chunk, chunk)
        return [
            pltpu.make_async_copy(
                source.at[piece, pl.ds(k * HD, HD)],
                wbuf.at[k, piece, pl.ds(part * HD, HD)],
                w_sem.at[k, c, part],
            )
            for part, source in enumerate((w_key, w_value))
        ]

    def patch_copy(c):
        piece = pl.ds(c * chunk, chunk)
        return pltpu.make_async_copy(store.at[:, :, piece], xbuf.at[:, :, piece], x_sem.at[c])

    small = [
        pltpu.make_async_copy(queries, qraw, q_sem.at[0]),
        pltpu.make_async_copy(query_gain, gains.at[0], q_sem.at[1]),
        pltpu.make_async_copy(key_gain, gains.at[1], q_sem.at[2]),
        pltpu.make_async_copy(owner_hbm, owner_table, q_sem.at[3]),
        pltpu.make_async_copy(reader_hbm, reader_table, q_sem.at[4]),
        pltpu.make_async_copy(request_hbm, request_image, q_sem.at[5]),
        pltpu.make_async_copy(tiles_hbm, image_tiles, q_sem.at[6]),
    ]
    for c in range(CHUNKS):
        for k in range(kv_local):
            for copy in weight_copies(k, c):
                copy.start()
        patch_copy(c).start()
        if c == 0:
            for copy in small:
                copy.start()

    for copy in small:
        copy.wait()
    gain = gains[0] * gains[1] * (1.0 / math.sqrt(HD))
    for h in range(kv_local * group):
        lanes = pl.ds(h * HD, HD)
        head = qraw[:, lanes].astype(jnp.float32)
        mean = jnp.mean(head * head, axis=-1, keepdims=True)
        qf[:, lanes] = head * lax.rsqrt(mean + EPSILON) * gain
    for k in range(kv_local):
        for t in range(n_depth):
            for g in range(group):
                qs[pl.ds(t * block + g * share, share), :] = qf[
                    pl.ds(t * share, share), pl.ds((k * group + g) * HD, HD)
                ]
        qx[wide, k] = qs[...].astype(jnp.bfloat16)
    row = lax.broadcasted_iota(jnp.int32, (group_rows, HD), 0)
    request = row // block * share + row % share
    entry = jnp.zeros((group_rows, HD), jnp.int32)
    for b in range(batch):
        entry = jnp.where(request == b, request_image[b], entry)
    qx[wide, kv_local] = entry.astype(jnp.float32).astype(jnp.bfloat16)

    def query_copy(offset):
        return pltpu.make_async_remote_copy(
            src_ref=qx.at[wide],
            dst_ref=qx.at[wide],
            send_sem=q_send.at[offset],
            recv_sem=q_recv.at[offset],
            device_id={"wide": lax.rem(wide + offset, n_wide)},
            device_id_type=MESH,
        )

    def query_landed(offset):
        source = lax.rem(wide + n_wide - offset, n_wide)
        return pltpu.make_async_remote_copy(
            src_ref=qx.at[source],
            dst_ref=qx.at[source],
            send_sem=q_send.at[offset],
            recv_sem=q_recv.at[offset],
            device_id={"wide": lax.rem(wide + offset, n_wide)},
            device_id_type=MESH,
        )

    def result_copy(offset):
        index, device = peer(offset)
        return pltpu.make_async_remote_copy(
            src_ref=msg.at[index],
            dst_ref=got.at[offset],
            send_sem=m_send.at[offset],
            recv_sem=m_recv.at[offset],
            device_id=device,
            device_id_type=MESH,
        )

    def send_results():
        def step(offset, carry):
            result_copy(offset).start()
            return carry

        lax.fori_loop(1, peers, step, 0, unroll=peers <= 8)

    whole_tiles = TILE_P % rows == 0

    def read_queries():
        for offset in range(1, n_wide):
            query_landed(offset).wait_recv()
        for g in range(n_wide):
            entry = qx[g, kv_local].astype(jnp.float32)
            slots = jnp.full((group_rows, HD), -1, jnp.int32)
            limits = jnp.zeros((group_rows, HD), jnp.int32)
            for r in range(reader_table.shape[1]):
                image = reader_table[g, r]
                slot = owner_table[image]
                limit = image_tiles[image] * TILE_P - depth * rows
                if whole_tiles:
                    slot = jnp.where(limit > 0, slot, -1)
                slots = jnp.where(entry == r, slot, slots)
                limits = jnp.where(entry == r, limit, limits)
            row_slot[pl.ds(g * group_rows, group_rows), :] = slots
            row_limit[pl.ds(g * group_rows, group_rows), :] = limits

    def wider(tile):
        return jnp.concatenate([tile] * (rows // HD), axis=1) if rows > HD else tile

    def prepare(k):
        total = raw[k]
        head = total[:, :HD]
        mean = jnp.mean(head * head, axis=-1, keepdims=True)
        keys[k] = (head * lax.rsqrt(mean + EPSILON)).astype(jnp.bfloat16)
        value = total[:, HD:].astype(jnp.bfloat16)
        values[k] = jnp.concatenate([value, jnp.ones_like(value)], axis=1)

    def attend_groups(k, start, count):
        span = pl.ds(start * group_rows, count * group_rows)
        asked = qx[pl.ds(start, count), k].reshape(count * group_rows, HD)
        wanted, limits = wider(row_slot[span, :]), wider(row_limit[span, :])
        scores = lax.dot_general(
            asked, keys[k], (((1,), (1,)), ((), ())), preferred_element_type=jnp.float32
        )
        weights = []
        for j in range(images):
            keep = wanted == wide * images + j
            if not whole_tiles:
                place = lax.broadcasted_iota(jnp.int32, keep.shape, 1)
                keep = keep & (place < limits)
            part = jnp.exp(scores[:, j * rows : (j + 1) * rows])
            weights.append(jnp.where(keep, part, 0.0).astype(jnp.bfloat16))
        total = jnp.dot(
            jnp.concatenate(weights, axis=1), values[k], preferred_element_type=jnp.float32
        )
        total = total.astype(jnp.bfloat16).reshape(count * n_depth, block, 2 * HD)
        dest = pl.ds(start * n_depth, count * n_depth)
        msg[dest, k] = total[:, :, :HD]
        below = total[:, :, HD:]
        if k:
            lane = lax.broadcasted_iota(jnp.int32, below.shape, 2)
            older = msg[dest, kv_local].astype(jnp.float32)
            below = jnp.where(lane < k * part_lanes, older, below.astype(jnp.float32))
        msg[dest, kv_local] = below.astype(jnp.bfloat16)

    def attend(k):
        if n_wide <= 2:
            attend_groups(k, 0, n_wide)
        else:

            def step(g, carry):
                attend_groups(k, g, 1)
                return carry

            lax.fori_loop(0, n_wide, step, 0)

    def project(k, c):
        piece = pl.ds(c * chunk, chunk)
        part = jnp.dot(
            xbuf[:, :, piece].reshape(images * rows, chunk),
            wbuf[k, piece, :],
            preferred_element_type=jnp.float32,
        )
        raw[k] = part if c == 0 else raw[k] + part

    for c in range(CHUNKS):
        for k in range(kv_local):
            for copy in weight_copies(k, c):
                copy.wait()
        patch_copy(c).wait()
        for k in range(kv_local):
            project(k, c)
            if c == CHUNKS - 1:
                prepare(k)
        if c == min(MEET, CHUNKS - 1):
            pl.semaphore_wait(barrier, peers - 1)
            for offset in range(1, n_wide):
                query_copy(offset).start()
    read_queries()
    for k in range(kv_local):
        attend(k)
    send_results()

    total = msg[me].astype(jnp.float32)

    def collect(offset, total):
        result_copy(offset).wait_recv()
        return total + got[offset].astype(jnp.float32)

    total = lax.fori_loop(1, peers, collect, total, unroll=peers <= 8)
    for k in range(kv_local):
        res[...] = total[k] / total[kv_local, :, k * part_lanes : k * part_lanes + 1]
        for g in range(group):
            out[:, pl.ds((k * group + g) * HD, HD)] = res[pl.ds(g * share, share), :].astype(
                out.dtype
            )

    for offset in range(1, n_wide):
        query_copy(offset).wait_send()

    def drain(offset, carry):
        result_copy(offset).wait_send()
        return carry

    lax.fori_loop(1, peers, drain, 0, unroll=peers <= 8)


def local(
    n_wide,
    n_depth,
    patch_store,
    w_key,
    w_value,
    key_gain,
    query_gain,
    queries,
    owner_table,
    reader_table,
    request_image,
    image_tiles,
):
    images, rows, width = patch_store.shape
    kv_local = w_key.shape[1] // HD
    batch, q_cols = queries.shape
    group = q_cols // (kv_local * HD)
    share = batch // n_depth
    block = share * group
    group_rows = n_depth * block
    peers = n_wide * n_depth
    total_rows = peers * block
    anywhere = pl.BlockSpec(memory_space=pl.ANY)
    dma = pltpu.SemaphoreType.DMA
    return pl.pallas_call(
        functools.partial(kernel, n_wide, n_depth),
        out_shape=pltpu.VMEM((share, q_cols), jnp.bfloat16),
        in_specs=[anywhere] * 10,
        out_specs=pl.BlockSpec(memory_space=pltpu.VMEM),
        scratch_shapes=[
            pltpu.SMEM(owner_table.shape, jnp.int32),
            pltpu.SMEM(reader_table.shape, jnp.int32),
            pltpu.SMEM(request_image.shape, jnp.int32),
            pltpu.SMEM(image_tiles.shape, jnp.int32),
            pltpu.VMEM((images, rows, width), jnp.bfloat16),
            pltpu.VMEM((kv_local, width, 2 * HD), jnp.bfloat16),
            pltpu.VMEM((batch, q_cols), jnp.bfloat16),
            pltpu.VMEM((2, 1, HD), jnp.float32),
            pltpu.VMEM((batch, q_cols), jnp.float32),
            pltpu.VMEM((group_rows, HD), jnp.float32),
            pltpu.VMEM((n_wide, kv_local + 1, group_rows, HD), jnp.bfloat16),
            pltpu.VMEM((total_rows, HD), jnp.int32),
            pltpu.VMEM((total_rows, HD), jnp.int32),
            pltpu.VMEM((kv_local, images * rows, 2 * HD), jnp.float32),
            pltpu.VMEM((kv_local, images * rows, HD), jnp.bfloat16),
            pltpu.VMEM((kv_local, images * rows, 2 * HD), jnp.bfloat16),
            pltpu.VMEM((peers, kv_local + 1, block, HD), jnp.bfloat16),
            pltpu.VMEM((peers, kv_local + 1, block, HD), jnp.bfloat16),
            pltpu.VMEM((block, HD), jnp.float32),
            dma((kv_local, CHUNKS, 2)),
            dma((CHUNKS,)),
            dma((7,)),
            dma((n_wide,)),
            dma((n_wide,)),
            dma((peers,)),
            dma((peers,)),
        ],
        compiler_params=pltpu.CompilerParams(
            collective_id=0, has_side_effects=True, vmem_limit_bytes=56 * 1024 * 1024
        ),
    )(
        patch_store,
        w_key,
        w_value,
        key_gain.reshape(1, HD),
        query_gain.reshape(1, HD),
        queries,
        owner_table,
        reader_table,
        request_image,
        image_tiles,
    )


def solution(mesh):
    placed = (
        P("wide", "depth", None),
        P(None, "narrow"),
        P(None, "narrow"),
        P(),
        P(),
        P("wide", "narrow"),
        P(),
        P(),
        P("wide"),
        P(),
    )
    return jax.shard_map(
        functools.partial(local, mesh.shape["wide"], mesh.shape["depth"]),
        mesh=mesh,
        in_specs=placed,
        out_specs=P(("wide", "depth"), "narrow"),
        check_vma=False,
    )
```

profile of v0, /device:TPU:0, one launch (start us, length us, event | category | flops | bytes accessed | tf_op | source)
XLA Modules:
  0.0 17.2 jit_solution(6190802467928955704)
XLA Ops:
  0.0 16.6 %shard_map.100 = bf16[4,1024]{1,0:T(4,128)(2,1)S(1)} custom-call(bf16[4,256,4096]{2,1,0:T(8,128)(2,1)} %store.1, bf16[4096,256]{1,0:T(8,128)(2,1)} %w_key.1, bf16[4096,256]{1,0:T(8,128)(2,1)} %w_value.1, f32[1,128]{1,0:T(1,128)} %bitcast.2, f32[1,128]{1,0:T(1,128)} %bitcast.3, bf16[16,1024]{1,0:T(8,128)(2,1)} %queries.1, s32[8]{0:T(128)} %owner_hbm.1, ...), custom_call_target="tpu_custom_call" | custom-call | tf_op jit(solution)/shard_map/pallas_call | solution.py:329
  16.6 0.6 %copy.12 = bf16[4,1024]{1,0:T(4,128)(2,1)} copy(bf16[4,1024]{1,0:T(4,128)(2,1)S(1)} %shard_map.100) | data formatting | bytes 16384
where the time goes:
time: 17.3 us; the launch traced here: 17.2 us
  Pallas kernels  16.6 us (96%)
  local copies, waits for them, and re-layouts  0.6 us (3%)
    pallas_call x1, Pallas kernels, local(): pl.pallas_call(functools.partial(kernel, n_wide, n_depth), out_shape=pltp...  16.6 us
    unnamed x1, local copies, waits for them, and re-layouts  0.6 us

commit v1 on v0

v1 whole, which is shorter than its diff:
```python
import functools
import math

import jax
import jax.numpy as jnp
from jax import lax
from jax.experimental import pallas as pl
from jax.experimental.pallas import tpu as pltpu
from jax.sharding import PartitionSpec as P

HD = 128
TILE_P = 256
EPSILON = 1e-05
MXU = 256
PIECE = 128
CHUNKS = (1, 1, 2, 4, 4, 4)
MEET = 1
MESH = pl.DeviceIdType.MESH


def kernel(
    n_wide,
    n_depth,
    store,
    w_key,
    w_value,
    key_gain,
    query_gain,
    queries,
    owner_hbm,
    reader_hbm,
    request_hbm,
    tiles_hbm,
    out,
    owner_table,
    reader_table,
    request_image,
    image_tiles,
    xbuf,
    wkbuf,
    wvbuf,
    qraw,
    gains,
    qf,
    qs,
    qx,
    row_slot,
    row_limit,
    keyed,
    valued,
    msg,
    got,
    res,
    w_sem,
    x_sem,
    q_sem,
    q_send,
    q_recv,
    m_send,
    m_recv,
):
    images, rows, width = xbuf.shape
    kv_local = wkbuf.shape[1] // HD
    batch = qraw.shape[0]
    group = qraw.shape[1] // (kv_local * HD)
    share = batch // n_depth
    block = share * group
    group_rows = n_depth * block
    peers = n_wide * n_depth
    span = PIECE // group_rows
    tiles = width // MXU
    pieces = rows // PIECE
    wide, depth = lax.axis_index("wide"), lax.axis_index("depth")
    me = wide * n_depth + depth
    part_lanes = HD // kv_local
    heads = range(kv_local)

    barrier = pltpu.get_barrier_semaphore()

    def peer(offset):
        there = {
            "wide": lax.rem(wide + offset // n_depth, n_wide),
            "depth": lax.rem(depth + offset % n_depth, n_depth),
        }
        return there["wide"] * n_depth + there["depth"], there

    small = [
        pltpu.make_async_copy(queries, qraw, q_sem.at[0]),
        pltpu.make_async_copy(query_gain, gains.at[0], q_sem.at[1]),
        pltpu.make_async_copy(key_gain, gains.at[1], q_sem.at[2]),
        pltpu.make_async_copy(owner_hbm, owner_table, q_sem.at[3]),
        pltpu.make_async_copy(reader_hbm, reader_table, q_sem.at[4]),
        pltpu.make_async_copy(request_hbm, request_image, q_sem.at[5]),
        pltpu.make_async_copy(tiles_hbm, image_tiles, q_sem.at[6]),
    ]

    starts = [sum(CHUNKS[:c]) for c in range(len(CHUNKS))]

    def chunk_copies(c):
        piece = pl.ds(starts[c] * MXU, CHUNKS[c] * MXU)
        return [
            pltpu.make_async_copy(w_key.at[piece, :], wkbuf.at[piece, :], w_sem.at[c, 0]),
            pltpu.make_async_copy(w_value.at[piece, :], wvbuf.at[piece, :], w_sem.at[c, 1]),
            pltpu.make_async_copy(store.at[:, :, piece], xbuf.at[:, :, piece], x_sem.at[c]),
        ]

    for copy in chunk_copies(0) + small:
        copy.start()
    for c in range(1, len(CHUNKS)):
        for copy in chunk_copies(c):
            copy.start()

    def greet(offset, carry):
        pl.semaphore_signal(barrier, inc=1, device_id=peer(offset)[1], device_id_type=MESH)
        return carry

    lax.fori_loop(1, peers, greet, 0, unroll=peers <= 8)

    def prepare_queries():
        gain = gains[0] * gains[1] * (1.0 / math.sqrt(HD))
        for h in range(kv_local * group):
            lanes = pl.ds(h * HD, HD)
            head = qraw[:, lanes].astype(jnp.float32)
            mean = jnp.mean(head * head, axis=-1, keepdims=True)
            qf[:, lanes] = head * lax.rsqrt(mean + EPSILON) * gain
        for k in heads:
            for t in range(n_depth):
                for g in range(group):
                    qs[pl.ds(t * block + g * share, share), :] = qf[
                        pl.ds(t * share, share), pl.ds((k * group + g) * HD, HD)
                    ]
            qx[wide, k] = qs[...].astype(jnp.bfloat16)
        row = lax.broadcasted_iota(jnp.int32, (group_rows, HD), 0)
        request = row // block * share + row % share
        entry = jnp.zeros((group_rows, HD), jnp.int32)
        for b in range(batch):
            entry = jnp.where(request == b, request_image[b], entry)
        qx[wide, kv_local] = entry.astype(jnp.float32).astype(jnp.bfloat16)

    def query_copy(offset):
        return pltpu.make_async_remote_copy(
            src_ref=qx.at[wide],
            dst_ref=qx.at[wide],
            send_sem=q_send.at[offset],
            recv_sem=q_recv.at[offset],
            device_id={"wide": lax.rem(wide + offset, n_wide)},
            device_id_type=MESH,
        )

    def query_landed(offset):
        source = lax.rem(wide + n_wide - offset, n_wide)
        return pltpu.make_async_remote_copy(
            src_ref=qx.at[source],
            dst_ref=qx.at[source],
            send_sem=q_send.at[offset],
            recv_sem=q_recv.at[offset],
            device_id={"wide": lax.rem(wide + offset, n_wide)},
            device_id_type=MESH,
        )

    def result_copy(offset):
        index, device = peer(offset)
        return pltpu.make_async_remote_copy(
            src_ref=msg.at[index],
            dst_ref=got.at[offset],
            send_sem=m_send.at[offset],
            recv_sem=m_recv.at[offset],
            device_id=device,
            device_id_type=MESH,
        )

    whole_tiles = TILE_P % rows == 0

    def read_queries():
        for offset in range(1, n_wide):
            query_landed(offset).wait_recv()
        for g in range(n_wide):
            entry = qx[g, kv_local].astype(jnp.float32)
            slots = jnp.full((group_rows, HD), -1, jnp.int32)
            limits = jnp.zeros((group_rows, HD), jnp.int32)
            for r in range(reader_table.shape[1]):
                image = reader_table[g, r]
                slot = owner_table[image]
                limit = image_tiles[image] * TILE_P - depth * rows
                if whole_tiles:
                    slot = jnp.where(limit > 0, slot, -1)
                slots = jnp.where(entry == r, slot, slots)
                limits = jnp.where(entry == r, limit, limits)
            row_slot[pl.ds(g * group_rows, group_rows), :] = slots
            row_limit[pl.ds(g * group_rows, group_rows), :] = limits

    def wider(tile):
        return jnp.concatenate([tile] * (rows // HD), axis=1) if rows > HD else tile

    def run(*flat):
        accs = [
            [flat[(k * images + j) * pieces : (k * images + j + 1) * pieces] for j in range(images)]
            for k in heads
        ]
        total = [accs[k][0][1] for k in heads]
        turn = [0]

        def next_register():
            turn[0] ^= 1
            return turn[0]

        def project(t, chosen):
            register = next_register()
            at = pl.ds(t * MXU, MXU)
            for k in heads:
                lanes = pl.ds(k * HD, HD)
                pltpu.matmul_push_rhs(
                    jnp.concatenate([wkbuf[at, lanes], wvbuf[at, lanes]], axis=1), register, k
                )
            first = True
            for j in chosen:
                for h in range(pieces):
                    patches = xbuf[j, pl.ds(h * PIECE, PIECE), at]
                    for k in heads:
                        pltpu.matmul_acc_lhs(accs[k][j][h], patches, register if first else None)
                    first = False

        def settle(k, j):
            raw = jnp.concatenate([pltpu.matmul_pop(acc) for acc in accs[k][j]], axis=0)
            head = raw[:, :HD]
            mean = jnp.mean(head * head, axis=-1, keepdims=True)
            key = (head * lax.rsqrt(mean + EPSILON)).astype(jnp.bfloat16)
            value = raw[:, HD:].astype(jnp.bfloat16)
            return jnp.concatenate([key, value], axis=1), jnp.concatenate(
                [value, jnp.ones_like(value)], axis=1
            )

        def asked(k, start):
            ask = qx[pl.ds(start, span), k].reshape(PIECE, HD)
            return jnp.concatenate([ask, jnp.zeros_like(ask)], axis=1)

        def weigh(k, j, wanted, limits):
            scores = pltpu.matmul_pop(accs[k][j][0])
            keep = wanted == wide * images + j
            if not whole_tiles:
                place = lax.broadcasted_iota(jnp.int32, keep.shape, 1)
                keep = keep & (place < limits)
            return jnp.where(keep, jnp.exp(scores), 0.0).astype(jnp.bfloat16)

        def finish(start, sums):
            dest = pl.ds(start * n_depth, span * n_depth)
            below = None
            for k in heads:
                both = sums[k].astype(jnp.bfloat16).reshape(span * n_depth, block, 2 * HD)
                msg[dest, k] = both[:, :, :HD]
                mine = sums[k][:, HD:]
                lane = lax.broadcasted_iota(jnp.int32, mine.shape, 1)
                below = mine if k == 0 else jnp.where(lane < k * part_lanes, below, mine)
            msg[dest, kv_local] = below.astype(jnp.bfloat16).reshape(span * n_depth, block, HD)

        for c in range(len(CHUNKS) - 1):
            if c == 0:
                for copy in small:
                    copy.wait()
            for copy in chunk_copies(c):
                copy.wait()
            for t in range(starts[c], starts[c] + CHUNKS[c]):
                project(t, range(images))
            if c == 0:
                prepare_queries()
            if c == MEET:
                pl.semaphore_wait(barrier, peers - 1)
                for offset in range(1, n_wide):
                    query_copy(offset).start()
        for copy in chunk_copies(len(CHUNKS) - 1):
            copy.wait()
        last = range(starts[-1], tiles)
        half = len(last) // 2
        if n_wide == span:
            read_queries()
            wanted, limits = wider(row_slot[...]), wider(row_limit[...])
            asks = [asked(k, 0) for k in heads]

            def stage_scores(j):
                register = next_register()
                for k in heads:
                    key, value = settle(k, j)
                    valued[k, j] = value
                    pltpu.matmul_push_rhs(key, register, k, transpose=True)
                    pltpu.matmul_acc_lhs(accs[k][j][0], asks[k], register)

            def stage_values(j):
                register = next_register()
                for k in heads:
                    weights = weigh(k, j, wanted, limits)
                    pltpu.matmul_push_rhs(valued[k, j], register, k)
                    pltpu.matmul_acc_lhs(total[k], weights, register)

            def stage_project(j, which):
                for t in which:
                    project(t, [j])

            for j in range(images):
                stage_project(j, last[:half])
                if j >= 2:
                    stage_values(j - 2)
                stage_project(j, last[half:])
                if j >= 1:
                    stage_scores(j - 1)
            stage_values(images - 2)
            stage_scores(images - 1)
            stage_values(images - 1)
            finish(0, [pltpu.matmul_pop(total[k]) for k in heads])
        else:
            for t in last:
                project(t, range(images))
            read_queries()
            for j in range(images):
                for k in heads:
                    keyed[k, j], valued[k, j] = settle(k, j)

            def attend(s, carry):
                start = s * span
                here = pl.ds(start * group_rows, PIECE)
                wanted, limits = wider(row_slot[here, :]), wider(row_limit[here, :])
                for j in range(images):
                    for k in heads:
                        pltpu.matmul_push_rhs(keyed[k, j], 0, k, transpose=True)
                        pltpu.matmul_acc_lhs(accs[k][j][0], asked(k, start), 0)
                for j in range(images):
                    for k in heads:
                        weights = weigh(k, j, wanted, limits)
                        pltpu.matmul_push_rhs(valued[k, j], 0, k)
                        pltpu.matmul_acc_lhs(total[k], weights, 0)
                finish(start, [pltpu.matmul_pop(total[k]) for k in heads])
                return carry

            lax.fori_loop(0, n_wide // span, attend, 0)

    pl.run_scoped(
        run,
        *[
            pltpu.ACC(k)((PIECE, MXU), jnp.float32)
            for k in heads
            for _ in range(images * pieces)
        ],
    )

    if peers <= 8:
        order = [
            a * n_depth + b
            for b in [*range(1, n_depth), 0]
            for a in [*range(1, n_wide), 0]
            if a or b
        ]
        for offset in order:
            result_copy(offset).start()
        total = msg[me].astype(jnp.float32)
        for offset in order[::-1]:
            result_copy(offset).wait_recv()
            total = total + got[offset].astype(jnp.float32)
    else:

        def step(offset, carry):
            result_copy(offset).start()
            return carry

        lax.fori_loop(1, peers, step, 0)

        def collect(offset, total):
            result_copy(offset).wait_recv()
            return total + got[offset].astype(jnp.float32)

        total = lax.fori_loop(1, peers, collect, msg[me].astype(jnp.float32))
    for k in heads:
        res[...] = total[k] / total[kv_local, :, k * part_lanes : k * part_lanes + 1]
        for g in range(group):
            out[:, pl.ds((k * group + g) * HD, HD)] = res[pl.ds(g * share, share), :].astype(
                out.dtype
            )

    for offset in range(1, n_wide):
        query_copy(offset).wait_send()

    def drain(offset, carry):
        result_copy(offset).wait_send()
        return carry

    lax.fori_loop(1, peers, drain, 0, unroll=peers <= 8)


def local(
    n_wide,
    n_depth,
    patch_store,
    w_key,
    w_value,
    key_gain,
    query_gain,
    queries,
    owner_table,
    reader_table,
    request_image,
    image_tiles,
):
    images, rows, width = patch_store.shape
    kv_local = w_key.shape[1] // HD
    batch, q_cols = queries.shape
    group = q_cols // (kv_local * HD)
    share = batch // n_depth
    block = share * group
    group_rows = n_depth * block
    peers = n_wide * n_depth
    total_rows = peers * block
    anywhere = pl.BlockSpec(memory_space=pl.ANY)
    dma = pltpu.SemaphoreType.DMA
    return pl.pallas_call(
        functools.partial(kernel, n_wide, n_depth),
        out_shape=pltpu.VMEM((share, q_cols), jnp.bfloat16),
        in_specs=[anywhere] * 10,
        out_specs=pl.BlockSpec(memory_space=pltpu.VMEM),
        scratch_shapes=[
            pltpu.SMEM(owner_table.shape, jnp.int32),
            pltpu.SMEM(reader_table.shape, jnp.int32),
            pltpu.SMEM(request_image.shape, jnp.int32),
            pltpu.SMEM(image_tiles.shape, jnp.int32),
            pltpu.VMEM((images, rows, width), jnp.bfloat16),
            pltpu.VMEM((width, kv_local * HD), jnp.bfloat16),
            pltpu.VMEM((width, kv_local * HD), jnp.bfloat16),
            pltpu.VMEM((batch, q_cols), jnp.bfloat16),
            pltpu.VMEM((2, 1, HD), jnp.float32),
            pltpu.VMEM((batch, q_cols), jnp.float32),
            pltpu.VMEM((group_rows, HD), jnp.float32),
            pltpu.VMEM((n_wide, kv_local + 1, group_rows, HD), jnp.bfloat16),
            pltpu.VMEM((total_rows, HD), jnp.int32),
            pltpu.VMEM((total_rows, HD), jnp.int32),
            pltpu.VMEM((kv_local, images, rows, 2 * HD), jnp.bfloat16),
            pltpu.VMEM((kv_local, images, rows, 2 * HD), jnp.bfloat16),
            pltpu.VMEM((peers, kv_local + 1, block, HD), jnp.bfloat16),
            pltpu.VMEM((peers, kv_local + 1, block, HD), jnp.bfloat16),
            pltpu.VMEM((block, HD), jnp.float32),
            dma((len(CHUNKS), 2)),
            dma((len(CHUNKS),)),
            dma((7,)),
            dma((n_wide,)),
            dma((n_wide,)),
            dma((peers,)),
            dma((peers,)),
        ],
        compiler_params=pltpu.CompilerParams(
            collective_id=0, has_side_effects=True, vmem_limit_bytes=56 * 1024 * 1024
        ),
    )(
        patch_store,
        w_key,
        w_value,
        key_gain.reshape(1, HD),
        query_gain.reshape(1, HD),
        queries,
        owner_table,
        reader_table,
        request_image,
        image_tiles,
    )


def solution(mesh):
    placed = (
        P("wide", "depth", None),
        P(None, "narrow"),
        P(None, "narrow"),
        P(),
        P(),
        P("wide", "narrow"),
        P(),
        P(),
        P("wide"),
        P(),
    )
    return jax.shard_map(
        functools.partial(local, mesh.shape["wide"], mesh.shape["depth"]),
        mesh=mesh,
        in_specs=placed,
        out_specs=P(("wide", "depth"), "narrow"),
        check_vma=False,
    )
```

time: 17.3 us -> 16.4 us (0.948)
  Pallas kernels: 16.6 us -> 15.6 us
    pallas_call x1, Pallas kernels: 16.6 us -> 15.6 us  [local(): pl.pallas_call(functools.partial(kernel, n_wide, n_depth), out_shape=pltp...]
where the time goes in v1:
time: 16.4 us; the launch traced here: 16.2 us
  Pallas kernels  15.6 us (95%)
  local copies, waits for them, and re-layouts  0.6 us (4%)
    pallas_call x1, Pallas kernels, local(): pl.pallas_call(functools.partial(kernel, n_wide, n_depth), out_shape=pltp...  15.6 us
    unnamed x1, local copies, waits for them, and re-layouts  0.6 us

profile of v1, /device:TPU:0, one launch (start us, length us, event | category | flops | bytes accessed | tf_op | source)
XLA Modules:
  0.0 16.2 jit_solution(6636395782707461993)
XLA Ops:
  0.0 15.6 %shard_map.100 = bf16[4,1024]{1,0:T(4,128)(2,1)S(1)} custom-call(bf16[4,256,4096]{2,1,0:T(8,128)(2,1)} %store.1, bf16[4096,256]{1,0:T(8,128)(2,1)} %w_key.1, bf16[4096,256]{1,0:T(8,128)(2,1)} %w_value.1, f32[1,128]{1,0:T(1,128)} %bitcast.2, f32[1,128]{1,0:T(1,128)} %bitcast.3, bf16[16,1024]{1,0:T(8,128)(2,1)} %queries.1, s32[8]{0:T(128)} %owner_hbm.1, ...), custom_call_target="tpu_custom_call" | custom-call | tf_op jit(solution)/shard_map/pallas_call | solution.py:412
  15.6 0.6 %copy.12 = bf16[4,1024]{1,0:T(4,128)(2,1)} copy(bf16[4,1024]{1,0:T(4,128)(2,1)S(1)} %shard_map.100) | data formatting | bytes 16384

commit v2 on v1

v2 whole, which is shorter than its diff:
```python
import functools
import math

import jax
import jax.numpy as jnp
from jax import lax
from jax.experimental import pallas as pl
from jax.experimental.pallas import tpu as pltpu
from jax.sharding import PartitionSpec as P

HD = 128
TILE_P = 256
EPSILON = 1e-05
MXU = 256
MXUS = 2
CHUNKS = (2, 2, 4, 4, 4)
AHEAD = 8
MEET = 0
MESH = pl.DeviceIdType.MESH


def kernel(
    n_wide,
    n_depth,
    store,
    w_key,
    w_value,
    key_gain,
    query_gain,
    queries,
    owner_hbm,
    reader_hbm,
    request_hbm,
    tiles_hbm,
    out,
    owner_table,
    reader_table,
    request_image,
    image_tiles,
    xbuf,
    wkbuf,
    wvbuf,
    qraw,
    gains,
    qf,
    qs,
    qx,
    row_slot,
    row_limit,
    keyed,
    valued,
    weighed,
    sums,
    msg,
    got,
    res,
    c_sem,
    q_sem,
    q_send,
    q_recv,
    m_send,
    m_recv,
):
    images, rows, width = xbuf.shape
    kv_local = wkbuf.shape[1] // HD
    batch = qraw.shape[0]
    group = qraw.shape[1] // (kv_local * HD)
    share = batch // n_depth
    block = share * group
    group_rows = n_depth * block
    peers = n_wide * n_depth
    asked_rows = MXU // kv_local
    span = asked_rows // group_rows
    tiles = width // MXU
    pairs = images // MXUS
    wide, depth = lax.axis_index("wide"), lax.axis_index("depth")
    me = wide * n_depth + depth
    part_lanes = HD // kv_local
    heads = range(kv_local)

    barrier = pltpu.get_barrier_semaphore()

    def peer(offset):
        there = {
            "wide": lax.rem(wide + offset // n_depth, n_wide),
            "depth": lax.rem(depth + offset % n_depth, n_depth),
        }
        return there["wide"] * n_depth + there["depth"], there

    small = [
        pltpu.make_async_copy(queries, qraw, q_sem.at[0]),
        pltpu.make_async_copy(query_gain, gains.at[0], q_sem.at[0]),
        pltpu.make_async_copy(key_gain, gains.at[1], q_sem.at[0]),
        pltpu.make_async_copy(owner_hbm, owner_table, q_sem.at[0]),
        pltpu.make_async_copy(reader_hbm, reader_table, q_sem.at[0]),
        pltpu.make_async_copy(request_hbm, request_image, q_sem.at[0]),
        pltpu.make_async_copy(tiles_hbm, image_tiles, q_sem.at[0]),
    ]

    starts = [sum(CHUNKS[:c]) for c in range(len(CHUNKS))]

    def chunk_copies(c):
        piece = pl.ds(starts[c] * MXU, CHUNKS[c] * MXU)
        return [
            [
                pltpu.make_async_copy(w_key.at[piece, :], wkbuf.at[piece, :], c_sem.at[c, 0]),
                pltpu.make_async_copy(store.at[:, :, piece], xbuf.at[:, :, piece], c_sem.at[c, 0]),
            ],
            [pltpu.make_async_copy(w_value.at[piece, :], wvbuf.at[piece, :], c_sem.at[c, 1])],
        ]

    def begin(copies):
        for copy in copies:
            copy.start()

    def end(copies):
        for copy in copies:
            copy.wait()

    begun = [0]

    def fetch(arrived):
        while begun[0] < len(CHUNKS):
            c = begun[0]
            if c and starts[c] + CHUNKS[c] > arrived + AHEAD:
                break
            keys_part, values_part = chunk_copies(c)
            begin(keys_part)
            if c == 0:
                begin(small)
            begin(values_part)
            begun[0] += 1

    fetch(0)

    def greet(offset, carry):
        pl.semaphore_signal(barrier, inc=1, device_id=peer(offset)[1], device_id_type=MESH)
        return carry

    lax.fori_loop(1, peers, greet, 0, unroll=peers <= 8)

    def prepare_queries():
        gain = gains[0] * gains[1] * (1.0 / math.sqrt(HD))
        for h in range(kv_local * group):
            lanes = pl.ds(h * HD, HD)
            head = qraw[:, lanes].astype(jnp.float32)
            mean = jnp.mean(head * head, axis=-1, keepdims=True)
            qf[:, lanes] = head * lax.rsqrt(mean + EPSILON) * gain
        for k in heads:
            for t in range(n_depth):
                for g in range(group):
                    qs[pl.ds(t * block + g * share, share), :] = qf[
                        pl.ds(t * share, share), pl.ds((k * group + g) * HD, HD)
                    ]
            qx[wide, k] = qs[...].astype(jnp.bfloat16)
        row = lax.broadcasted_iota(jnp.int32, (group_rows, HD), 0)
        request = row // block * share + row % share
        entry = jnp.zeros((group_rows, HD), jnp.int32)
        for b in range(batch):
            entry = jnp.where(request == b, request_image[b], entry)
        qx[wide, kv_local] = entry.astype(jnp.float32).astype(jnp.bfloat16)

    def query_copy(offset):
        return pltpu.make_async_remote_copy(
            src_ref=qx.at[wide],
            dst_ref=qx.at[wide],
            send_sem=q_send.at[offset - 1],
            recv_sem=q_recv.at[offset - 1],
            device_id={"wide": lax.rem(wide + offset, n_wide)},
            device_id_type=MESH,
        )

    def query_landed(offset):
        source = lax.rem(wide + n_wide - offset, n_wide)
        return pltpu.make_async_remote_copy(
            src_ref=qx.at[source],
            dst_ref=qx.at[source],
            send_sem=q_send.at[offset - 1],
            recv_sem=q_recv.at[offset - 1],
            device_id={"wide": lax.rem(wide + offset, n_wide)},
            device_id_type=MESH,
        )

    def result_copy(offset):
        index, device = peer(offset)
        return pltpu.make_async_remote_copy(
            src_ref=msg.at[index],
            dst_ref=got.at[offset - 1],
            send_sem=m_send.at[0],
            recv_sem=m_recv.at[0],
            device_id=device,
            device_id_type=MESH,
        )

    def all_results():
        every = pl.ds(0, peers - 1)
        return pltpu.make_async_remote_copy(
            src_ref=msg.at[every],
            dst_ref=got.at[every],
            send_sem=m_send.at[0],
            recv_sem=m_recv.at[0],
            device_id=peer(1)[1],
            device_id_type=MESH,
        )

    whole_tiles = TILE_P % rows == 0

    def read_queries():
        for offset in range(1, n_wide):
            query_landed(offset).wait_recv()
        for g in range(n_wide):
            entry = qx[g, kv_local].astype(jnp.float32)
            slots = jnp.full((group_rows, HD), -1, jnp.int32)
            limits = jnp.zeros((group_rows, HD), jnp.int32)
            for r in range(reader_table.shape[1]):
                image = reader_table[g, r]
                slot = owner_table[image]
                limit = image_tiles[image] * TILE_P - depth * rows
                if whole_tiles:
                    slot = jnp.where(limit > 0, slot, -1)
                slots = jnp.where(entry == r, slot, slots)
                limits = jnp.where(entry == r, limit, limits)
            row_slot[pl.ds(g * group_rows, group_rows), :] = slots
            row_limit[pl.ds(g * group_rows, group_rows), :] = limits

    def wider(tile):
        return jnp.concatenate([tile] * (rows // HD), axis=1) if rows > HD else tile

    def run(*flat):
        accs = [flat[2 * j : 2 * j + 2] for j in range(images)]
        mine = [range(m * pairs, (m + 1) * pairs) for m in range(MXUS)]
        total = [accs[mine[m][0]][0] for m in range(MXUS)]
        turn = [0]

        def next_register():
            turn[0] ^= 1
            return turn[0]

        def project(t, part, chosen):
            register = next_register()
            at = pl.ds(t * MXU, MXU)
            weight = (wkbuf, wvbuf)[part][at, :]
            for m in range(MXUS):
                pltpu.matmul_push_rhs(weight, register, m)
            first = True
            for i in chosen:
                for m in range(MXUS):
                    j = mine[m][i]
                    pltpu.matmul_acc_lhs(
                        accs[j][part], xbuf[j, :, at], register if first else None
                    )
                first = False

        def settle_keys(j):
            raw = pltpu.matmul_pop(accs[j][0])
            done = []
            for k in heads:
                head = raw[:, k * HD : (k + 1) * HD]
                mean = jnp.mean(head * head, axis=-1, keepdims=True)
                done.append((head * lax.rsqrt(mean + EPSILON)).astype(jnp.bfloat16))
            return jnp.concatenate(done, axis=1)

        def settle_values(j):
            return pltpu.matmul_pop(accs[j][1]).astype(jnp.bfloat16)

        def asked(start):
            lines = []
            for k in heads:
                ask = qx[pl.ds(start, span), k].reshape(asked_rows, HD)
                none = jnp.zeros_like(ask)
                lines.append(jnp.concatenate([ask if k == i else none for i in heads], axis=1))
            return jnp.concatenate(lines, axis=0)

        def weigh(j, wanted, limits):
            scores = pltpu.matmul_pop(accs[j][0])
            keep = wanted == wide * images + j
            if not whole_tiles:
                place = lax.broadcasted_iota(jnp.int32, keep.shape, 1)
                keep = keep & (place < limits)
            keep = jnp.concatenate([keep] * kv_local, axis=0)
            weights = jnp.where(keep, jnp.exp(scores), 0.0)
            weighed[j] = weights.astype(jnp.bfloat16)
            lanes = weights[:, :HD]
            for at in range(HD, rows, HD):
                lanes = lanes + weights[:, at : at + HD]
            return lanes

        def send_denominators(start):
            dest = pl.ds(start * n_depth, span * n_depth)
            below = jnp.sum(sums[...], axis=-1, keepdims=True)
            lane = lax.broadcasted_iota(jnp.int32, (asked_rows, HD), 1)
            plane = jnp.broadcast_to(below[:asked_rows], (asked_rows, HD))
            for k in heads[1:]:
                plane = jnp.where(
                    lane < k * part_lanes, plane, below[k * asked_rows : (k + 1) * asked_rows]
                )
            msg[dest, kv_local] = plane.astype(jnp.bfloat16).reshape(span * n_depth, block, HD)

        def finish(start):
            dest = pl.ds(start * n_depth, span * n_depth)
            both = [pltpu.matmul_pop(total[m]) for m in range(MXUS)]
            for k in heads:
                line, lanes = slice(k * asked_rows, (k + 1) * asked_rows), slice(k * HD, (k + 1) * HD)
                number = both[0][line, lanes]
                for m in range(1, MXUS):
                    number = number + both[m][line, lanes]
                msg[dest, k] = number.astype(jnp.bfloat16).reshape(span * n_depth, block, HD)

        for c in range(len(CHUNKS) - 1):
            if c == 0:
                end(small)
            for part in range(2):
                end(chunk_copies(c)[part])
                if part == 0:
                    fetch(starts[c] + CHUNKS[c])
                for t in range(starts[c], starts[c] + CHUNKS[c]):
                    project(t, part, range(pairs))
                if c == 0 and part == 0:
                    prepare_queries()
            if c == MEET:
                pl.semaphore_wait(barrier, peers - 1)
                for offset in range(1, n_wide):
                    query_copy(offset).start()
        keys_last, values_last = chunk_copies(len(CHUNKS) - 1)
        end(keys_last)
        last = range(starts[-1], tiles)
        half = len(last) // 2

        def stage_scores(i, ask):
            register = next_register()
            for m in range(MXUS):
                j = mine[m][i]
                pltpu.matmul_push_rhs(settle_keys(j), register, m, transpose=True)
                pltpu.matmul_acc_lhs(accs[j][0], ask, register)

        def stage_weights(i, wanted, limits):
            for m in range(MXUS):
                lanes = weigh(mine[m][i], wanted, limits)
                if i == 0 and m == 0:
                    sums[...] = lanes
                else:
                    sums[...] += lanes

        def stage_values(i):
            register = next_register()
            for m in range(MXUS):
                j = mine[m][i]
                pltpu.matmul_push_rhs(settle_values(j), register, m)
                pltpu.matmul_acc_lhs(total[m], weighed[j], register)

        def stage_project(i, part, which):
            for t in which:
                project(t, part, [i])

        if n_wide == span:
            read_queries()
            wanted, limits = wider(row_slot[...]), wider(row_limit[...])
            ask = asked(0)
            for i in range(pairs):
                stage_project(i, 0, last)
            end(values_last)
            for i in range(pairs):
                stage_project(i, 1, last[:half])
                if i > 0:
                    stage_weights(i - 1, wanted, limits)
                    stage_values(i - 1)
                stage_project(i, 1, last[half:]) if i + 1 < pairs else None
                stage_scores(i, ask)
                if i + 1 == pairs:
                    stage_project(i, 1, last[half:])
            stage_weights(pairs - 1, wanted, limits)
            send_denominators(0)
            stage_values(pairs - 1)
            finish(0)
        else:
            end(values_last)
            for t in last:
                for part in range(2):
                    project(t, part, range(pairs))
            read_queries()
            for j in range(images):
                keyed[j], valued[j] = settle_keys(j), settle_values(j)

            def attend(s, carry):
                start = s * span
                here = pl.ds(start * group_rows, asked_rows)
                wanted, limits = wider(row_slot[here, :]), wider(row_limit[here, :])
                ask = asked(start)
                for i in range(pairs):
                    for m in range(MXUS):
                        j = mine[m][i]
                        pltpu.matmul_push_rhs(keyed[j], 0, m, transpose=True)
                        pltpu.matmul_acc_lhs(accs[j][0], ask, 0)
                for i in range(pairs):
                    stage_weights(i, wanted, limits)
                for i in range(pairs):
                    for m in range(MXUS):
                        j = mine[m][i]
                        pltpu.matmul_push_rhs(valued[j], 0, m)
                        pltpu.matmul_acc_lhs(total[m], weighed[j], 0)
                send_denominators(start)
                finish(start)
                return carry

            lax.fori_loop(0, n_wide // span, attend, 0)

    pl.run_scoped(
        run,
        *[
            pltpu.ACC(j // pairs)((rows, MXU), jnp.float32)
            for j in range(images)
            for _ in range(2)
        ],
    )

    if peers <= 8:
        order = [
            a * n_depth + b
            for b in [*range(1, n_depth), 0]
            for a in [*range(1, n_wide), 0]
            if a or b
        ]
        for offset in order:
            result_copy(offset).start()
    else:

        def step(offset, carry):
            result_copy(offset).start()
            return carry

        lax.fori_loop(1, peers, step, 0)

    total = msg[me].astype(jnp.float32)
    all_results().wait_recv()

    def collect(offset, total):
        return total + got[offset - 1].astype(jnp.float32)

    total = lax.fori_loop(1, peers, collect, total, unroll=peers <= 8)
    for k in heads:
        res[...] = total[k] / total[kv_local, :, k * part_lanes : k * part_lanes + 1]
        for g in range(group):
            out[:, pl.ds((k * group + g) * HD, HD)] = res[pl.ds(g * share, share), :].astype(
                out.dtype
            )

    for offset in range(1, n_wide):
        query_copy(offset).wait_send()

    all_results().wait_send()


def local(
    n_wide,
    n_depth,
    patch_store,
    w_key,
    w_value,
    key_gain,
    query_gain,
    queries,
    owner_table,
    reader_table,
    request_image,
    image_tiles,
):
    images, rows, width = patch_store.shape
    kv_local = w_key.shape[1] // HD
    batch, q_cols = queries.shape
    group = q_cols // (kv_local * HD)
    share = batch // n_depth
    block = share * group
    group_rows = n_depth * block
    peers = n_wide * n_depth
    total_rows = peers * block
    anywhere = pl.BlockSpec(memory_space=pl.ANY)
    dma = pltpu.SemaphoreType.DMA
    return pl.pallas_call(
        functools.partial(kernel, n_wide, n_depth),
        out_shape=pltpu.VMEM((share, q_cols), jnp.bfloat16),
        in_specs=[anywhere] * 10,
        out_specs=pl.BlockSpec(memory_space=pltpu.VMEM),
        scratch_shapes=[
            pltpu.SMEM(owner_table.shape, jnp.int32),
            pltpu.SMEM(reader_table.shape, jnp.int32),
            pltpu.SMEM(request_image.shape, jnp.int32),
            pltpu.SMEM(image_tiles.shape, jnp.int32),
            pltpu.VMEM((images, rows, width), jnp.bfloat16),
            pltpu.VMEM((width, kv_local * HD), jnp.bfloat16),
            pltpu.VMEM((width, kv_local * HD), jnp.bfloat16),
            pltpu.VMEM((batch, q_cols), jnp.bfloat16),
            pltpu.VMEM((2, 1, HD), jnp.float32),
            pltpu.VMEM((batch, q_cols), jnp.float32),
            pltpu.VMEM((group_rows, HD), jnp.float32),
            pltpu.VMEM((n_wide, kv_local + 1, group_rows, HD), jnp.bfloat16),
            pltpu.VMEM((total_rows, HD), jnp.int32),
            pltpu.VMEM((total_rows, HD), jnp.int32),
            pltpu.VMEM((images, rows, kv_local * HD), jnp.bfloat16),
            pltpu.VMEM((images, rows, kv_local * HD), jnp.bfloat16),
            pltpu.VMEM((images, MXU, rows), jnp.bfloat16),
            pltpu.VMEM((MXU, HD), jnp.float32),
            pltpu.VMEM((peers, kv_local + 1, block, HD), jnp.bfloat16),
            pltpu.VMEM((peers - 1, kv_local + 1, block, HD), jnp.bfloat16),
            pltpu.VMEM((block, HD), jnp.float32),
            dma((len(CHUNKS), 2)),
            dma((1,)),
            dma((n_wide - 1,)),
            dma((n_wide - 1,)),
            dma((1,)),
            dma((1,)),
        ],
        compiler_params=pltpu.CompilerParams(
            collective_id=0, has_side_effects=True, vmem_limit_bytes=56 * 1024 * 1024
        ),
    )(
        patch_store,
        w_key,
        w_value,
        key_gain.reshape(1, HD),
        query_gain.reshape(1, HD),
        queries,
        owner_table,
        reader_table,
        request_image,
        image_tiles,
    )


def solution(mesh):
    placed = (
        P("wide", "depth", None),
        P(None, "narrow"),
        P(None, "narrow"),
        P(),
        P(),
        P("wide", "narrow"),
        P(),
        P(),
        P("wide"),
        P(),
    )
    return jax.shard_map(
        functools.partial(local, mesh.shape["wide"], mesh.shape["depth"]),
        mesh=mesh,
        in_specs=placed,
        out_specs=P(("wide", "depth"), "narrow"),
        check_vma=False,
    )
```

time: 16.4 us -> 15.8 us (0.963)
  Pallas kernels: 15.6 us -> 15.1 us
    pallas_call x1, Pallas kernels: 15.6 us -> 15.1 us  [local(): pl.pallas_call(functools.partial(kernel, n_wide, n_depth), out_shape=pltp...]
where the time goes in v2:
time: 15.8 us; the launch traced here: 15.7 us
  Pallas kernels  15.1 us (96%)
  local copies, waits for them, and re-layouts  0.6 us (4%)
    pallas_call x1, Pallas kernels, local(): pl.pallas_call(functools.partial(kernel, n_wide, n_depth), out_shape=pltp...  15.1 us
    unnamed x1, local copies, waits for them, and re-layouts  0.6 us

profile of v2, /device:TPU:0, one launch (start us, length us, event | category | flops | bytes accessed | tf_op | source)
XLA Modules:
  0.0 15.7 jit_solution(2430977134862193504)
XLA Ops:
  0.0 15.1 %shard_map.100 = bf16[4,1024]{1,0:T(4,128)(2,1)S(1)} custom-call(bf16[4,256,4096]{2,1,0:T(8,128)(2,1)} %store.1, bf16[4096,256]{1,0:T(8,128)(2,1)} %w_key.1, bf16[4096,256]{1,0:T(8,128)(2,1)} %w_value.1, f32[1,128]{1,0:T(1,128)} %bitcast.2, f32[1,128]{1,0:T(1,128)} %bitcast.3, bf16[16,1024]{1,0:T(8,128)(2,1)} %queries.1, s32[8]{0:T(128)} %owner_hbm.1, ...), custom_call_target="tpu_custom_call" | custom-call | tf_op jit(solution)/shard_map/pallas_call | solution.py:478
  15.1 0.6 %copy.12 = bf16[4,1024]{1,0:T(4,128)(2,1)} copy(bf16[4,1024]{1,0:T(4,128)(2,1)S(1)} %shard_map.100) | data formatting | bytes 16384

commit v3 on v2

--- a/solution.py
+++ b/solution.py
@@ -99,14 +99,16 @@
 
     starts = [sum(CHUNKS[:c]) for c in range(len(CHUNKS))]
 
+    final = len(CHUNKS) - 1
+
     def chunk_copies(c):
         piece = pl.ds(starts[c] * MXU, CHUNKS[c] * MXU)
         return [
-            [
-                pltpu.make_async_copy(w_key.at[piece, :], wkbuf.at[piece, :], c_sem.at[c, 0]),
-                pltpu.make_async_copy(store.at[:, :, piece], xbuf.at[:, :, piece], c_sem.at[c, 0]),
-            ],
-            [pltpu.make_async_copy(w_value.at[piece, :], wvbuf.at[piece, :], c_sem.at[c, 1])],
+            pltpu.make_async_copy(w_key.at[piece, :], wkbuf.at[piece, :], c_sem.at[c]),
+            pltpu.make_async_copy(store.at[:, :, piece], xbuf.at[:, :, piece], c_sem.at[c]),
+            pltpu.make_async_copy(
+                w_value.at[piece, :], wvbuf.at[piece, :], c_sem.at[c]
+            ),
         ]
 
     def begin(copies):
@@ -124,11 +126,9 @@
             c = begun[0]
             if c and starts[c] + CHUNKS[c] > arrived + AHEAD:
                 break
-            keys_part, values_part = chunk_copies(c)
-            begin(keys_part)
+            begin(chunk_copies(c))
             if c == 0:
                 begin(small)
-            begin(values_part)
             begun[0] += 1
 
     fetch(0)
@@ -227,32 +227,53 @@
         return jnp.concatenate([tile] * (rows // HD), axis=1) if rows > HD else tile
 
     def run(*flat):
-        accs = [flat[2 * j : 2 * j + 2] for j in range(images)]
-        mine = [range(m * pairs, (m + 1) * pairs) for m in range(MXUS)]
-        total = [accs[mine[m][0]][0] for m in range(MXUS)]
-        turn = [0]
-
-        def next_register():
-            turn[0] ^= 1
-            return turn[0]
-
-        def project(t, part, chosen):
-            register = next_register()
-            at = pl.ds(t * MXU, MXU)
-            weight = (wkbuf, wvbuf)[part][at, :]
-            for m in range(MXUS):
-                pltpu.matmul_push_rhs(weight, register, m)
-            first = True
-            for i in chosen:
-                for m in range(MXUS):
-                    j = mine[m][i]
-                    pltpu.matmul_acc_lhs(
-                        accs[j][part], xbuf[j, :, at], register if first else None
-                    )
-                first = False
-
-        def settle_keys(j):
-            raw = pltpu.matmul_pop(accs[j][0])
+        accs = [flat[MXUS * j : MXUS * (j + 1)] for j in range(images)]
+        total = [accs[0][0], accs[pairs][1]]
+        turn = [0] * MXUS
+        ready = []
+
+        def push(tile, m, transpose=False):
+            turn[m] ^= 1
+            pltpu.matmul_push_rhs(tile, turn[m], m, transpose=transpose)
+            return turn[m]
+
+        def push_weights(step):
+            ready.append(
+                [
+                    push((wkbuf, wvbuf)[part][pl.ds(t * MXU, MXU), :], m)
+                    for m, (part, t) in enumerate(step[0])
+                ]
+            )
+
+        def project(steps, after=None):
+            if not ready:
+                push_weights(steps[0])
+            for n, (weights, rounds) in enumerate(steps):
+                registers = ready.pop()
+                for first, (j, slots) in enumerate(rounds):
+                    patches = {}
+                    for m, (part, t) in enumerate(weights):
+                        if t not in patches:
+                            patches[t] = xbuf[j, :, pl.ds(t * MXU, MXU)]
+                        pltpu.matmul_acc_lhs(
+                            slots[m], patches[t], None if first else registers[m]
+                        )
+                following = steps[n + 1] if n + 1 < len(steps) else after
+                if following:
+                    push_weights(following)
+
+        def together(t, chosen):
+            return [(0, t), (1, t)], [(j, accs[j]) for j in chosen]
+
+        def apart(part, j, t, u):
+            slots = [accs[j][0], accs[j - pairs if part == 0 else j][1]]
+            return [(part, t), (part, u)], [(j, slots)]
+
+        def popped(slots):
+            return functools.reduce(jnp.add, [pltpu.matmul_pop(slot) for slot in slots])
+
+        def settle_keys(slots):
+            raw = popped(slots)
             done = []
             for k in heads:
                 head = raw[:, k * HD : (k + 1) * HD]
@@ -260,8 +281,8 @@
                 done.append((head * lax.rsqrt(mean + EPSILON)).astype(jnp.bfloat16))
             return jnp.concatenate(done, axis=1)
 
-        def settle_values(j):
-            return pltpu.matmul_pop(accs[j][1]).astype(jnp.bfloat16)
+        def settle_values(slots):
+            return popped(slots).astype(jnp.bfloat16)
 
         def asked(start):
             lines = []
@@ -271,8 +292,8 @@
                 lines.append(jnp.concatenate([ask if k == i else none for i in heads], axis=1))
             return jnp.concatenate(lines, axis=0)
 
-        def weigh(j, wanted, limits):
-            scores = pltpu.matmul_pop(accs[j][0])
+        def weigh(j, slot, wanted, limits):
+            scores = pltpu.matmul_pop(slot)
             keep = wanted == wide * images + j
             if not whole_tiles:
                 place = lax.broadcasted_iota(jnp.int32, keep.shape, 1)
@@ -306,98 +327,105 @@
                     number = number + both[m][line, lanes]
                 msg[dest, k] = number.astype(jnp.bfloat16).reshape(span * n_depth, block, HD)
 
-        for c in range(len(CHUNKS) - 1):
+        def chunk_steps(c, chosen):
+            return [together(t, chosen) for t in range(starts[c], starts[c] + CHUNKS[c])]
+
+        def stage_scores(m, slot, key, ask):
+            register = push(key, m, transpose=True)
+            pltpu.matmul_acc_lhs(slot, ask, register)
+
+        def stage_weights(j, slot, wanted, limits, first):
+            lanes = weigh(j, slot, wanted, limits)
+            if first:
+                sums[...] = lanes
+            else:
+                sums[...] += lanes
+
+        def stage_values(m, j, value):
+            register = push(value, m)
+            pltpu.matmul_acc_lhs(total[m], weighed[j], register)
+
+        early, late = range(pairs), range(pairs, images)
+        for c in range(final):
+            end(chunk_copies(c))
             if c == 0:
                 end(small)
-            for part in range(2):
-                end(chunk_copies(c)[part])
-                if part == 0:
-                    fetch(starts[c] + CHUNKS[c])
-                for t in range(starts[c], starts[c] + CHUNKS[c]):
-                    project(t, part, range(pairs))
-                if c == 0 and part == 0:
-                    prepare_queries()
+            fetch(starts[c] + CHUNKS[c])
+            project(chunk_steps(c, range(images)))
+            if c == 0:
+                prepare_queries()
             if c == MEET:
                 pl.semaphore_wait(barrier, peers - 1)
                 for offset in range(1, n_wide):
                     query_copy(offset).start()
-        keys_last, values_last = chunk_copies(len(CHUNKS) - 1)
-        end(keys_last)
-        last = range(starts[-1], tiles)
-        half = len(last) // 2
-
-        def stage_scores(i, ask):
-            register = next_register()
-            for m in range(MXUS):
-                j = mine[m][i]
-                pltpu.matmul_push_rhs(settle_keys(j), register, m, transpose=True)
-                pltpu.matmul_acc_lhs(accs[j][0], ask, register)
-
-        def stage_weights(i, wanted, limits):
-            for m in range(MXUS):
-                lanes = weigh(mine[m][i], wanted, limits)
-                if i == 0 and m == 0:
-                    sums[...] = lanes
-                else:
-                    sums[...] += lanes
-
-        def stage_values(i):
-            register = next_register()
-            for m in range(MXUS):
-                j = mine[m][i]
-                pltpu.matmul_push_rhs(settle_values(j), register, m)
-                pltpu.matmul_acc_lhs(total[m], weighed[j], register)
-
-        def stage_project(i, part, which):
-            for t in which:
-                project(t, part, [i])
-
+        end(chunk_copies(final))
+        half = CHUNKS[final] // 2
         if n_wide == span:
+
+            def apart_steps(part, j):
+                return [
+                    apart(part, j, t, t + half) for t in range(starts[final], starts[final] + half)
+                ]
+
+            steps = []
+            for j in early:
+                steps += chunk_steps(final, [j])
+            project(steps)
+            for j in early:
+                valued[j] = settle_values([accs[j][1]])
+                keyed[j] = settle_keys([accs[j][0]])
+            steps = []
+            for j in late:
+                steps += apart_steps(0, j)
+            project(steps)
             read_queries()
             wanted, limits = wider(row_slot[...]), wider(row_limit[...])
             ask = asked(0)
-            for i in range(pairs):
-                stage_project(i, 0, last)
-            end(values_last)
-            for i in range(pairs):
-                stage_project(i, 1, last[:half])
-                if i > 0:
-                    stage_weights(i - 1, wanted, limits)
-                    stage_values(i - 1)
-                stage_project(i, 1, last[half:]) if i + 1 < pairs else None
-                stage_scores(i, ask)
-                if i + 1 == pairs:
-                    stage_project(i, 1, last[half:])
-            stage_weights(pairs - 1, wanted, limits)
-            send_denominators(0)
-            stage_values(pairs - 1)
+            for n, (i, j) in enumerate(zip(early, late)):
+                last_one = n + 1 == pairs
+                slot = accs[j - pairs][1]
+                stage_scores(0, accs[i][0], keyed[i], ask)
+                if last_one:
+                    stage_scores(1, slot, settle_keys([accs[j][0], slot]), ask)
+                    project(apart_steps(1, j)[: half // 2])
+                    for p in early[:-1]:
+                        stage_weights(p, accs[p][0], wanted, limits, p == 0)
+                        stage_values(0, p, valued[p])
+                    project(apart_steps(1, j)[half // 2 :])
+                else:
+                    key = settle_keys([accs[j][0], slot])
+                    project(apart_steps(1, j))
+                    stage_scores(1, slot, key, ask)
+            stage_weights(early[-1], accs[early[-1]][0], wanted, limits, pairs == 1)
+            stage_values(0, early[-1], valued[early[-1]])
+            for j in late:
+                stage_weights(j, accs[j - pairs][1], wanted, limits, False)
+                if j == late[-1]:
+                    send_denominators(0)
+                stage_values(1, j, settle_values(accs[j]))
             finish(0)
         else:
-            end(values_last)
-            for t in last:
-                for part in range(2):
-                    project(t, part, range(pairs))
+            project(chunk_steps(final, range(images)))
             read_queries()
             for j in range(images):
-                keyed[j], valued[j] = settle_keys(j), settle_values(j)
+                keyed[j], valued[j] = settle_keys([accs[j][0]]), settle_values([accs[j][1]])
 
             def attend(s, carry):
                 start = s * span
                 here = pl.ds(start * group_rows, asked_rows)
                 wanted, limits = wider(row_slot[here, :]), wider(row_limit[here, :])
                 ask = asked(start)
-                for i in range(pairs):
-                    for m in range(MXUS):
-                        j = mine[m][i]
-                        pltpu.matmul_push_rhs(keyed[j], 0, m, transpose=True)
-                        pltpu.matmul_acc_lhs(accs[j][0], ask, 0)
-                for i in range(pairs):
-                    stage_weights(i, wanted, limits)
-                for i in range(pairs):
-                    for m in range(MXUS):
-                        j = mine[m][i]
-                        pltpu.matmul_push_rhs(valued[j], 0, m)
-                        pltpu.matmul_acc_lhs(total[m], weighed[j], 0)
+                for j in range(images):
+                    m, i = divmod(j, pairs)
+                    pltpu.matmul_push_rhs(keyed[j], 0, m, transpose=True)
+                    pltpu.matmul_acc_lhs(accs[i][m], ask, 0)
+                for j in range(images):
+                    m, i = divmod(j, pairs)
+                    stage_weights(j, accs[i][m], wanted, limits, j == 0)
+                for j in range(images):
+                    m = j // pairs
+                    pltpu.matmul_push_rhs(valued[j], 0, m)
+                    pltpu.matmul_acc_lhs(total[m], weighed[j], 0)
                 send_denominators(start)
                 finish(start)
                 return carry
@@ -407,9 +435,9 @@
     pl.run_scoped(
         run,
         *[
-            pltpu.ACC(j // pairs)((rows, MXU), jnp.float32)
-            for j in range(images)
-            for _ in range(2)
+            pltpu.ACC(m)((rows, MXU), jnp.float32)
+            for _ in range(images)
+            for m in range(MXUS)
         ],
     )
 
@@ -502,7 +530,7 @@
             pltpu.VMEM((peers, kv_local + 1, block, HD), jnp.bfloat16),
             pltpu.VMEM((peers - 1, kv_local + 1, block, HD), jnp.bfloat16),
             pltpu.VMEM((block, HD), jnp.float32),
-            dma((len(CHUNKS), 2)),
+            dma((len(CHUNKS),)),
             dma((1,)),
             dma((n_wide - 1,)),
             dma((n_wide - 1,)),

time: 15.8 us -> 15.6 us (0.987)
  Pallas kernels: 15.1 us -> 14.8 us
    pallas_call x1, Pallas kernels: 15.1 us -> 14.8 us  [local(): pl.pallas_call(functools.partial(kernel, n_wide, n_depth), out_shape=pltp...]
where the time goes in v3:
time: 15.6 us; the launch traced here: 15.4 us
  Pallas kernels  14.8 us (95%)
  local copies, waits for them, and re-layouts  0.6 us (4%)
    pallas_call x1, Pallas kernels, local(): pl.pallas_call(functools.partial(kernel, n_wide, n_depth), out_shape=pltp...  14.8 us
    unnamed x1, local copies, waits for them, and re-layouts  0.6 us

profile of v3, /device:TPU:0, one launch (start us, length us, event | category | flops | bytes accessed | tf_op | source)
XLA Modules:
  0.0 15.4 jit_solution(11502442939223785411)
XLA Ops:
  0.0 14.8 %shard_map.100 = bf16[4,1024]{1,0:T(4,128)(2,1)S(1)} custom-call(bf16[4,256,4096]{2,1,0:T(8,128)(2,1)} %store.1, bf16[4096,256]{1,0:T(8,128)(2,1)} %w_key.1, bf16[4096,256]{1,0:T(8,128)(2,1)} %w_value.1, f32[1,128]{1,0:T(1,128)} %bitcast.2, f32[1,128]{1,0:T(1,128)} %bitcast.3, bf16[16,1024]{1,0:T(8,128)(2,1)} %queries.1, s32[8]{0:T(128)} %owner_hbm.1, ...), custom_call_target="tpu_custom_call" | custom-call | tf_op jit(solution)/shard_map/pallas_call | solution.py:506
  14.8 0.6 %copy.12 = bf16[4,1024]{1,0:T(4,128)(2,1)} copy(bf16[4,1024]{1,0:T(4,128)(2,1)S(1)} %shard_map.100) | data formatting | bytes 16384

commit v4 on v3

--- a/solution.py
+++ b/solution.py
@@ -58,7 +58,6 @@
     q_sem,
     q_send,
     q_recv,
-    m_send,
     m_recv,
 ):
     images, rows, width = xbuf.shape
@@ -104,10 +103,10 @@
     def chunk_copies(c):
         piece = pl.ds(starts[c] * MXU, CHUNKS[c] * MXU)
         return [
-            pltpu.make_async_copy(w_key.at[piece, :], wkbuf.at[piece, :], c_sem.at[c]),
-            pltpu.make_async_copy(store.at[:, :, piece], xbuf.at[:, :, piece], c_sem.at[c]),
+            pltpu.make_async_copy(w_key.at[piece, :], wkbuf.at[piece, :], c_sem.at[c % 3]),
+            pltpu.make_async_copy(store.at[:, :, piece], xbuf.at[:, :, piece], c_sem.at[c % 3]),
             pltpu.make_async_copy(
-                w_value.at[piece, :], wvbuf.at[piece, :], c_sem.at[c]
+                w_value.at[piece, :], wvbuf.at[piece, :], c_sem.at[c % 3]
             ),
         ]
 
@@ -186,7 +185,7 @@
         return pltpu.make_async_remote_copy(
             src_ref=msg.at[index],
             dst_ref=got.at[offset - 1],
-            send_sem=m_send.at[0],
+            send_sem=q_sem.at[0],
             recv_sem=m_recv.at[0],
             device_id=device,
             device_id_type=MESH,
@@ -197,7 +196,7 @@
         return pltpu.make_async_remote_copy(
             src_ref=msg.at[every],
             dst_ref=got.at[every],
-            send_sem=m_send.at[0],
+            send_sem=q_sem.at[0],
             recv_sem=m_recv.at[0],
             device_id=peer(1)[1],
             device_id_type=MESH,
@@ -530,11 +529,10 @@
             pltpu.VMEM((peers, kv_local + 1, block, HD), jnp.bfloat16),
             pltpu.VMEM((peers - 1, kv_local + 1, block, HD), jnp.bfloat16),
             pltpu.VMEM((block, HD), jnp.float32),
-            dma((len(CHUNKS),)),
+            dma((3,)),
             dma((1,)),
             dma((n_wide - 1,)),
             dma((n_wide - 1,)),
-            dma((1,)),
             dma((1,)),
         ],
         compiler_params=pltpu.CompilerParams(

time: 15.6 us -> 15.6 us (level)
  no operation moved by 1% of the time
where the time goes in v4:
time: 15.6 us; the launch traced here: 15.4 us
  Pallas kernels  14.8 us (95%)
  local copies, waits for them, and re-layouts  0.6 us (4%)
    pallas_call x1, Pallas kernels, local(): pl.pallas_call(functools.partial(kernel, n_wide, n_depth), out_shape=pltp...  14.8 us
    unnamed x1, local copies, waits for them, and re-layouts  0.6 us

profile of v4, /device:TPU:0, one launch (start us, length us, event | category | flops | bytes accessed | tf_op | source)
XLA Modules:
  0.0 15.4 jit_solution(18042888756202856442)
XLA Ops:
  0.0 14.8 %shard_map.100 = bf16[4,1024]{1,0:T(4,128)(2,1)S(1)} custom-call(bf16[4,256,4096]{2,1,0:T(8,128)(2,1)} %store.1, bf16[4096,256]{1,0:T(8,128)(2,1)} %w_key.1, bf16[4096,256]{1,0:T(8,128)(2,1)} %w_value.1, f32[1,128]{1,0:T(1,128)} %bitcast.2, f32[1,128]{1,0:T(1,128)} %bitcast.3, bf16[16,1024]{1,0:T(8,128)(2,1)} %queries.1, s32[8]{0:T(128)} %owner_hbm.1, ...), custom_call_target="tpu_custom_call" | custom-call | tf_op jit(solution)/shard_map/pallas_call | solution.py:505
  14.8 0.6 %copy.12 = bf16[4,1024]{1,0:T(4,128)(2,1)} copy(bf16[4,1024]{1,0:T(4,128)(2,1)S(1)} %shard_map.100) | data formatting | bytes 16384
